TPU v7x, 32 devices: a whole 2x2x4 slice. The times are simulated.
32 devices in a mesh: group: 8 (over z, y), local: 4 (over x, core).
Axes of the slice: x: 2, y: 2, z: 4, core: 2. Of those that a mesh axis runs over, the one named last changes fastest.
Arguments:
- dense_vec: bfloat16 [4096, 128], P(('group', 'local')), may hold values from -6 to 6
- q_tables: float32 [1024, 26, 128], P('group'), may hold values from -4 to 4
- r_tables: float32 [256, 26, 128], P('local'), may hold values from -4 to 4
- owner: int32 [4096, 26, 1], P(('group', 'local')), may hold values from 0 to 7; in each aligned block of 3328 rows (0 to 3327, 3328 to 6655, ..., all dimensions but the last counted through in order) at most 832 rows name the same one
- q_local: int32 [4096, 26], P(('group', 'local')), may hold values from 0 to 127
- r_index: int32 [4096, 26], P(('group', 'local')), may hold values from 0 to 255
- w_one: bfloat16 [479, 1024], replicated, may hold values from -0.25 to 0.25
- b_one: float32 [1024], replicated, may hold values from -3 to 3
- w_two: bfloat16 [1024, 1024], replicated, may hold values from -0.1875 to 0.1875
- b_two: float32 [1024], replicated, may hold values from -3 to 3
- w_three: bfloat16 [1024, 512], replicated, may hold values from -0.1875 to 0.1875
- b_three: float32 [512], replicated, may hold values from -3 to 3
- w_four: bfloat16 [512, 256], replicated, may hold values from -0.25 to 0.25
- b_four: float32 [256], replicated, may hold values from -3 to 3
- cotangent: bfloat16 [4096, 256], P(('group', 'local')), may hold values from -6 to 6
Outputs:
- q_new: float32 [1024, 26, 128], P('group')
- r_new: float32 [256, 26, 128], P('local')
- w_one_new: float32 [479, 1024], replicated
- b_one_new: float32 [1024], replicated
- w_two_new: float32 [1024, 1024], replicated
- b_two_new: float32 [1024], replicated
- w_three_new: float32 [1024, 512], replicated
- b_three_new: float32 [512], replicated
- w_four_new: float32 [512, 256], replicated
- b_four_new: float32 [256], replicated
Inputs may be any that keep to these rules, and one draw needn't show every extreme that they name: `owner`: within the rows of one device (its 128 samples times 26 tables), no group is named more than 832 times, a bound that some block reaches.
All inputs are finite; a program needn't handle non-finite values.
Results may differ from a plain program's by a relative error of at most 0.0025.
Values may be sent and summed in bfloat16 or wider, within the bound.
A program may use at most 128 MiB of HBM per device.

v0:
```python
import jax
import jax.numpy as jnp
import numpy as np
from jax import lax
from jax.sharding import PartitionSpec as P

table_rate = 0.05
dense_rate = 0.0005


def silu_slope(preact):
    sigma = jax.nn.sigmoid(preact)
    return sigma * (1.0 + preact * (1.0 - sigma))


def interact(dense_rows, embeds):
    vectors_all = jnp.concatenate([dense_rows[:, None, :], embeds], axis=1).astype(jnp.float32)
    gram_mat = jnp.einsum("bid,bjd->bij", vectors_all, vectors_all, precision=lax.Precision.HIGHEST)
    lower_i, lower_j = np.tril_indices(vectors_all.shape[1], -1)
    pair_vals = gram_mat[:, lower_i, lower_j]
    features = jnp.concatenate([dense_rows.astype(jnp.float32), pair_vals], axis=1).astype(
        jnp.bfloat16
    )
    return (vectors_all, features)


def pair_back(d_pairs, vectors_all):
    vectors = vectors_all.shape[1]
    lower_i, lower_j = np.tril_indices(vectors, -1)
    spread = (
        jnp.zeros((vectors_all.shape[0], vectors, vectors), jnp.float32)
        .at[:, lower_i, lower_j]
        .set(d_pairs)
    )
    spread = spread + jnp.swapaxes(spread, 1, 2)
    return jnp.einsum("bij,bjd->bid", spread, vectors_all, precision=lax.Precision.HIGHEST)


def contract_rows(left, right):
    return lax.dot_general(
        left, right, (((0,), (0,)), ((), ())), preferred_element_type=jnp.float32
    )


def dense_pass(features, layers, cot_rows):
    inputs_list = [features]
    pre_list = []
    current = features
    for layer_idx, (weight, biases) in enumerate(layers):
        pre_act = jnp.dot(current, weight, preferred_element_type=jnp.float32) + biases
        pre_list.append(pre_act)
        if layer_idx + 1 < len(layers):
            current = jax.nn.silu(pre_act).astype(jnp.bfloat16)
            inputs_list.append(current)
    grad_low = cot_rows
    grad_full = cot_rows.astype(jnp.float32)
    grads = []
    back_grad = None
    for layer_idx in reversed(range(len(layers))):
        weight = layers[layer_idx][0]
        w_grad = contract_rows(inputs_list[layer_idx], grad_low)
        b_grad = jnp.sum(grad_full, axis=0)
        back_grad = lax.dot_general(
            grad_low, weight, (((1,), (1,)), ((), ())), preferred_element_type=jnp.float32
        )
        grads.insert(0, (w_grad, b_grad))
        if layer_idx > 0:
            grad_full = back_grad * silu_slope(pre_list[layer_idx - 1])
            grad_low = grad_full.astype(jnp.bfloat16)
    return (grads, back_grad)


def body(
    dense_vec,
    q_tables,
    r_tables,
    owner,
    q_local,
    r_index,
    w_one,
    b_one,
    w_two,
    b_two,
    w_three,
    b_three,
    w_four,
    b_four,
    cotangent,
):
    layers = [(w_one, b_one), (w_two, b_two), (w_three, b_three), (w_four, b_four)]
    groups = lax.axis_size("group")
    batch_rows, table_count = q_local.shape
    embed_width = q_tables.shape[2]
    lookups = batch_rows * table_count
    capacity = 2 * lookups // groups
    slot_count = groups * capacity
    segment_count = q_tables.shape[0] * table_count
    table_ids = jnp.arange(table_count, dtype=jnp.int32)[None, :]
    highest = lax.Precision.HIGHEST
    dest_group = owner[:, :, 0]
    owner_hits = (
        dest_group[:, :, None] == jnp.arange(groups, dtype=jnp.int32)[None, None, :]
    ).astype(jnp.float32)
    table_lower = (jnp.arange(table_count)[:, None] < jnp.arange(table_count)[None, :]).astype(
        jnp.float32
    )
    sample_lower = (jnp.arange(batch_rows)[:, None] < jnp.arange(batch_rows)[None, :]).astype(
        jnp.float32
    )
    within = jnp.einsum("st,bsg->btg", table_lower, owner_hits, precision=highest)
    before = jnp.einsum("cb,cg->bg", sample_lower, jnp.sum(owner_hits, axis=1), precision=highest)
    slot_rank = jnp.sum((within + before[:, None, :]) * owner_hits, axis=2).astype(jnp.int32)
    position = (dest_group * capacity + slot_rank).reshape(lookups)
    source = (
        jnp.full((slot_count,), lookups, jnp.int32)
        .at[position]
        .set(jnp.arange(lookups, dtype=jnp.int32))
    )
    row_keys = (q_local * table_count + table_ids).reshape(lookups)
    keys_padded = jnp.concatenate([row_keys, jnp.zeros((1,), jnp.int32)])
    outgoing = keys_padded[source].reshape(groups, capacity)
    flat_table = q_tables.reshape(segment_count, embed_width)
    request = lax.all_to_all(outgoing, "group", split_axis=0, concat_axis=0, tiled=True)
    served_rows = flat_table[request].astype(jnp.bfloat16)
    arrived = lax.all_to_all(served_rows, "group", split_axis=0, concat_axis=0, tiled=True)
    q_rows = arrived.reshape(slot_count, embed_width)[position]
    full_r = lax.all_gather(r_tables, "local", axis=0, tiled=True)
    remainder_count = full_r.shape[0]
    r_pick = (
        r_index[:, :, None] == jnp.arange(remainder_count, dtype=jnp.int32)[None, None, :]
    ).astype(jnp.float32)
    r_rows = jnp.einsum("btr,rtd->btd", r_pick, full_r, precision=highest).reshape(
        lookups, embed_width
    )
    q_val = q_rows.astype(jnp.float32)
    embeds = (q_val * r_rows).astype(jnp.bfloat16).reshape(batch_rows, table_count, embed_width)
    vectors_all, features = interact(dense_vec, embeds)
    grads, d_features = dense_pass(features, layers, cotangent)
    d_embed = pair_back(d_features[:, embed_width:], vectors_all)[:, 1:, :].reshape(
        lookups, embed_width
    )
    grad_padded = jnp.concatenate(
        [d_embed * r_rows, jnp.zeros((1, embed_width), jnp.float32)], axis=0
    )
    outbound = grad_padded[source].reshape(groups, capacity, embed_width)
    returned = (
        lax.all_to_all(
            outbound.astype(jnp.bfloat16), "group", split_axis=0, concat_axis=0, tiled=True
        )
        .astype(outbound.dtype)
        .reshape(slot_count, embed_width)
    )
    served_flat = request.reshape(slot_count)
    q_part = jax.ops.segment_sum(returned, served_flat, num_segments=segment_count).reshape(
        q_tables.shape
    )
    q_piece = lax.psum_scatter(
        q_part.astype(jnp.bfloat16), "local", scatter_dimension=0, tiled=True
    ).astype(jnp.float32)
    quarter = q_piece.shape[0]
    own_rows = lax.dynamic_slice_in_dim(q_tables, lax.axis_index("local") * quarter, quarter, 0)
    q_new = lax.all_gather(own_rows - table_rate * q_piece, "local", axis=0, tiled=True)
    r_part = jnp.einsum(
        "btr,btd->rtd",
        r_pick,
        (d_embed * q_val).reshape(batch_rows, table_count, embed_width),
        precision=highest,
    )
    summed = lax.psum(r_part, ("group", "local"))
    r_grad = lax.dynamic_slice_in_dim(
        summed, lax.axis_index("local") * r_tables.shape[0], r_tables.shape[0], 0
    )
    r_new = r_tables - table_rate * r_grad
    grad_wa, grad_ba, grad_wb, grad_bb, grad_wc, grad_bc, grad_wd, grad_bd = lax.psum(
        (
            grads[0][0],
            grads[0][1],
            grads[1][0],
            grads[1][1],
            grads[2][0],
            grads[2][1],
            grads[3][0],
            grads[3][1],
        ),
        ("group", "local"),
    )
    summed_grads = [(grad_wa, grad_ba), (grad_wb, grad_bb), (grad_wc, grad_bc), (grad_wd, grad_bd)]
    updated = []
    for (weight, biases), (w_grad, b_grad) in zip(layers, summed_grads):
        updated.append(weight.astype(jnp.float32) - dense_rate * w_grad)
        updated.append(biases - dense_rate * b_grad)
    return (
        q_new,
        r_new,
        updated[0],
        updated[1],
        updated[2],
        updated[3],
        updated[4],
        updated[5],
        updated[6],
        updated[7],
    )


def solution(mesh):
    return jax.shard_map(
        body,
        mesh=mesh,
        in_specs=(
            P(("group", "local"), None),
            P("group", None, None),
            P("local", None, None),
            P(("group", "local"), None, None),
            P(("group", "local"), None),
            P(("group", "local"), None),
            P(),
            P(),
            P(),
            P(),
            P(),
            P(),
            P(),
            P(),
            P(("group", "local"), None),
        ),
        out_specs=(
            P("group", None, None),
            P("local", None, None),
            P(),
            P(),
            P(),
            P(),
            P(),
            P(),
            P(),
            P(),
        ),
        check_vma=False,
    )
```

profile of v0, /device:TPU:0, one launch (start us, length us, event | category | flops | bytes accessed | tf_op | source)
XLA Modules:
  0.0 590.5 jit_solution(14401636984354006459)
XLA Ops:
  11.3 12.8 %scatter_custom_fusion = s32[6656]{0:T(1024)S(1)} fusion(s32[3328]{0:T(1024)S(1)} %fusion.38, s32[3328]{0:T(1024)S(1)} %iota.29, s32[]{:T(128)} %constant.27.clone.1), kind=kCustom, calls=%fused_computation.84 | custom fusion | bytes 26628 | tf_op jit(solution)/shard_map/scatter | solution.py:117
  24.1 34.5 %gather_fusion = s32[6656]{0:T(1024)S(1)} fusion(s32[3329]{0:T(1024)S(1)} %pad_add_fusion, s32[7168]{0:T(1024)S(1)} %pad_clamp_fusion.1), kind=kCustom, calls=%fused_computation | custom fusion | bytes 79872 | tf_op jit(solution)/shard_map/gather | solution.py:121
  59.4 7.3 %all-to-all-start = ((s32[8,1,832]{2,1,0:T(1,128)}), s32[8,1,832]{2,1,0:T(1,128)S(1)}, u32[]{:S(2)}, u32[]{:S(2)}) async-start(s32[8,1,832]{2,1,0:T(1,128)} %all_to_all.14), calls=%async_computation | async-start | bytes 57344 | tf_op jit(solution)/shard_map/all_to_all | solution.py:123
  66.7 2.5 copy.64
  69.4 4.0 all-to-all-done
  73.5 14.3 %gather_fusion.1 = bf16[6656,128]{1,0:T(8,128)(2,1)} fusion(bf16[3328,128]{1,0:T(8,128)(2,1)S(1)} %reshape.127, s32[7168]{0:T(1024)S(1)} %pad_clamp_fusion), kind=kCustom, calls=%fused_computation.1 | custom fusion | bytes 3434496 | tf_op jit(solution)/shard_map/gather | solution.py:124
  87.8 3.8 all-to-all-start.1
  91.7 38.3 %all-to-all-done.1 = bf16[8,832,128]{2,1,0:T(8,128)(2,1)S(1)} async-done(((bf16[8,832,128]{2,1,0:T(8,128)(2,1)}), bf16[8,832,128]{2,1,0:T(8,128)(2,1)S(1)}, u32[]{:S(2)}, u32[]{:S(2)}) %all-to-all-start.1) | async-done | bytes 1703968 | tf_op jit(solution)/shard_map/all_to_all | solution.py:125
  130.0 6.5 %gather_fusion.2 = bf16[3328,128]{1,0:T(8,128)(2,1)S(1)} fusion(bf16[6656,128]{1,0:T(8,128)(2,1)S(1)} %bitcast.53, s32[4096]{0:T(1024)S(1)} %pad_clamp_fusion.2), kind=kCustom, calls=%fused_computation.2 | custom fusion | bytes 1717248 | tf_op jit(solution)/shard_map/gather | solution.py:126
  137.2 7.3 %fusion.5 = (bf16[128,26,128]{2,0,1:T(8,128)(2,1)S(1)}, f32[26,128,128]{2,1,0:T(8,128)}) fusion(f32[128,26,128]{2,1,0:T(8,128)S(1)} %reshape.131, f32[256,26,128]{2,0,1:T(8,128)} %all-gather.3.cloned.1.call-done, s32[128,26]{0,1:T(8,128)S(1)} %copy-done.28), kind=kOutput, calls=%fused_computation.19 | convolution fusion | flops 1310326784 | bytes 7681024 | tf_op jit(solution)/shard_map/btr,rtd->btd/dot_general | solution.py:132
  146.4 4.9 gather_fusion.3
  152.9 2.3 convolution_add_fusion.1
  160.7 19.0 %scatter_fusion = f32[128,27,27]{0,2,1:T(8,128)S(1)} fusion(f32[128,27,27]{0,2,1:T(8,128)S(1)} %broadcast_in_dim.21, s32[351]{0:T(512)S(1)} %copy-done, f32[351,128]{1,0:T(8,128)S(1)} %convolution_bitcast_fusion), kind=kCustom, calls=%fused_computation.6 | custom fusion | bytes 541944 | tf_op jit(solution)/shard_map/scatter | solution.py:33
  180.0 2.9 copy.87
  182.9 3.3 fusion.14
  190.2 15.5 %gather_fusion.4 = bf16[6656,128]{1,0:T(8,128)(2,1)} fusion(bf16[3329,128]{1,0:T(8,128)(2,1)S(1)} %concatenate.24, s32[7168]{0:T(1024)} %copy-done.22), kind=kCustom, calls=%fused_computation.4 | custom fusion | bytes 3434496 | tf_op jit(solution)/shard_map/gather | solution.py:145
  205.7 4.4 all-to-all-start.2
  210.3 39.2 %all-to-all-done.2 = bf16[8,832,128]{2,1,0:T(8,128)(2,1)} async-done(((bf16[8,832,128]{2,1,0:T(8,128)(2,1)}), bf16[8,832,128]{2,1,0:T(8,128)(2,1)}, u32[]{:S(2)}, u32[]{:S(2)}) %all-to-all-start.2) | async-done | bytes 1703968 | tf_op jit(solution)/shard_map/all_to_all | solution.py:147
  249.5 40.3 %scatter_custom_fusion.2 = f32[3328,128]{1,0:T(8,128)} fusion(s32[6656]{0:T(1024)S(1)} %reshape.188, bf16[6656,128]{1,0:T(8,128)(2,1)} %bitcast.13, f32[]{:T(128)} %constant.24.clone.1), kind=kCustom, calls=%fused_computation.9 | custom fusion | flops 1703936 | bytes 3407876 | tf_op jit(solution)/shard_map/scatter-add | solution.py:154
  292.7 2.1 fusion.20
  296.5 1.8 fusion.28
  298.3 2.8 fusion.24
  301.1 6.2 %fusion.4 = f32[256,26,128]{0,2,1:T(8,128)} fusion(s32[128,26]{0,1:T(8,128)S(1)} %copy-done.28, f32[128,26,128]{2,1,0:T(8,128)S(1)} %fusion.14, f32[128,26,128]{2,1,0:T(8,128)S(1)} %copy-done.2), kind=kOutput, calls=%fused_computation.16 | convolution fusion | flops 1309900800 | bytes 6829056 | tf_op jit(solution)/shard_map/btr,btd->rtd/dot_general | solution.py:163
  307.3 14.6 %reduce-scatter.2.cloned.1.call-done = bf16[32,26,128]{2,1,0:T(8,128)(2,1)} async-done(((bf16[128,26,128]{2,1,0:T(8,128)(2,1)}), bf16[32,26,128]{2,1,0:T(8,128)(2,1)}) %reduce-scatter.2.cloned.1.call-update) | async-done | bytes 213008 | tf_op jit(solution)/shard_map/reduce_scatter | solution.py:157
  324.8 40.8 %all-reduce.1 = (f32[1024]{0:T(1024)S(1)}, f32[1024]{0:T(1024)S(1)}, f32[512]{0:T(512)S(1)}, f32[256]{0:T(256)S(1)}) all-reduce(f32[1024]{0:T(1024)S(1)} %copy-done.34, f32[1024]{0:T(1024)S(1)} %copy-done.33, f32[512]{0:T(512)S(1)} %copy-done.37, f32[256]{0:T(256)S(1)} %convert_reduce_fusion), channel_id=1, replica_groups=mesh['group'=8,'local'=4] {'group','local'}, use_global_device_ids=true, to_apply=%region_9.10 | all-reduce | flops 2816 | bytes 22528 | tf_op jit(solution)/shard_map/psum | solution.py:174
  367.4 192.2 %all-reduce.5.cloned.1.call-done = (f32[256,26,128]{0,2,1:T(8,128)}, f32[479,1024]{1,0:T(8,128)}, f32[1024,1024]{1,0:T(8,128)}, f32[1024,512]{1,0:T(8,128)}, f32[512,256]{1,0:T(8,128)}) async-done(((f32[256,26,128]{0,2,1:T(8,128)}, f32[479,1024]{1,0:T(8,128)}, f32[1024,1024]{1,0:T(8,128)}, f32[1024,512]{1,0:T(8,128)}, f32[512,256]{1,0:T(8,128)}), (f32[256,26,128]{0,2,1:T(8,128)}, f32[479,1024]{1,0:T(8,128)}, ...) | async-done | bytes 12185616 | tf_op jit(solution)/shard_map/psum | solution.py:169
  559.5 2.0 multiply_subtract_fusion.3
  562.9 1.9 multiply_subtract_fusion.4
  564.8 3.4 multiply_subtract_fusion.2
  571.3 2.7 multiply_subtract_fusion
  574.0 7.2 %all-gather.5.cloned.1.call-done = f32[128,26,128]{2,0,1:T(8,128)} async-done(((f32[32,26,128]{2,0,1:T(8,128)}), f32[128,26,128]{2,0,1:T(8,128)}) %all-gather.5.cloned.1.call-update) | async-done | bytes 1703952 | tf_op jit(solution)/shard_map/all_gather | solution.py:162
  581.2 2.8 copy.112
  (145 shorter events, 32.8 us)
Async XLA Ops:
  7.2 129.6 %all-gather.3.cloned.1.call-start = ((), (), s32[]{:S(2)}) async-start(), calls=%async_computation.4 | async-start | bytes 4259840 | tf_op jit(solution)/shard_map/all_gather | solution.py:127
  24.1 34.6 %copy-start.22 = (s32[7168]{0:T(1024)}, s32[7168]{0:T(1024)S(1)}, u32[]{:S(2)}) copy-start(s32[7168]{0:T(1024)S(1)} %pad_clamp_fusion.1) | copy-start | bytes 86020
  59.4 14.0 %all-to-all-start = ((s32[8,1,832]{2,1,0:T(1,128)}), s32[8,1,832]{2,1,0:T(1,128)S(1)}, u32[]{:S(2)}, u32[]{:S(2)}) async-start(s32[8,1,832]{2,1,0:T(1,128)} %all_to_all.14), calls=%async_computation | async-start | bytes 57344 | tf_op jit(solution)/shard_map/all_to_all | solution.py:123
  69.1 18.6 %copy-start.3 = (f32[128,26,128]{2,1,0:T(8,128)}, f32[128,26,128]{2,1,0:T(8,128)S(1)}, u32[]{:S(2)}) copy-start(f32[128,26,128]{2,1,0:T(8,128)S(1)} %copy.64) | copy-start | bytes 5111812
  73.3 14.4 %copy-start.23 = (s32[8,1,832]{2,1,0:T(1,128)}, s32[8,1,832]{2,1,0:T(1,128)S(1)}, u32[]{:S(2)}) copy-start(s32[8,1,832]{2,1,0:T(1,128)S(1)} %all-to-all-done) | copy-start | bytes 79876
  87.8 3.8 copy-start.25
  87.8 42.2 %all-to-all-start.1 = ((bf16[8,832,128]{2,1,0:T(8,128)(2,1)}), bf16[8,832,128]{2,1,0:T(8,128)(2,1)S(1)}, u32[]{:S(2)}, u32[]{:S(2)}) async-start(bf16[8,832,128]{2,1,0:T(8,128)(2,1)} %bitcast.55), calls=%async_computation.1 | async-start | bytes 3407872 | tf_op jit(solution)/shard_map/all_to_all | solution.py:125
  136.7 7.8 %copy-start.1 = (f32[128,26,128]{2,1,0:T(8,128)}, f32[128,26,128]{2,1,0:T(8,128)S(1)}, u32[]{:S(2)}) copy-start(f32[128,26,128]{2,1,0:T(8,128)S(1)} %reshape.131) | copy-start | bytes 5111812
  144.6 6.7 %copy-start.31 = (f32[1024]{0:T(1024)S(1)}, f32[1024]{0:T(1024)}, u32[]{:S(2)}) copy-start(f32[1024]{0:T(1024)} %param.30) | copy-start | bytes 12292
  145.3 7.6 %copy-start.32 = (f32[1024]{0:T(1024)S(1)}, f32[1024]{0:T(1024)}, u32[]{:S(2)}) copy-start(f32[1024]{0:T(1024)} %param.32) | copy-start | bytes 12292
  152.8 5.4 copy-start.11
  152.8 2.3 copy-start.14
  157.1 3.1 copy-start.26
  160.3 19.4 %copy-start.20 = (bf16[128,1024]{1,0:T(8,128)(2,1)}, bf16[128,1024]{1,0:T(8,128)(2,1)S(1)}, u32[]{:S(2)}) copy-start(bf16[128,1024]{1,0:T(8,128)(2,1)S(1)} %get-tuple-element.52) | copy-start | bytes 786436
  182.9 3.3 copy-start.4
  205.7 4.5 copy-start.24
  205.7 43.8 %all-to-all-start.2 = ((bf16[8,832,128]{2,1,0:T(8,128)(2,1)}), bf16[8,832,128]{2,1,0:T(8,128)(2,1)}, u32[]{:S(2)}, u32[]{:S(2)}) async-start(bf16[8,832,128]{2,1,0:T(8,128)(2,1)} %bitcast.54), calls=%async_computation.2 | async-start | bytes 3407872 | tf_op jit(solution)/shard_map/all_to_all | solution.py:147
  210.1 111.8 %reduce-scatter.2.cloned.1.call-start = ((), (), s32[]{:S(2)}) async-start(), calls=%async_computation.5 | async-start | bytes 1310720 | tf_op jit(solution)/shard_map/reduce_scatter | solution.py:157
  292.6 3.9 copy-start.18
  292.6 3.9 copy-start.27
  292.6 266.9 %all-reduce.5.cloned.1.call-start = ((), (), s32[]{:S(2)}) async-start(), calls=%async_computation.7 | async-start | bytes 24379392 | tf_op jit(solution)/shard_map/psum | solution.py:169
  294.8 3.5 copy-start.12
  298.3 2.8 copy-start.2
  307.3 16.9 %copy-start.8 = (f32[64,26,128]{2,0,1:T(8,128)S(1)}, f32[64,26,128]{2,0,1:T(8,128)}, u32[]{:S(2)}) copy-start(f32[64,26,128]{2,0,1:T(8,128)} %param.25) | copy-start | bytes 2555908
  307.3 273.9 %all-gather.5.cloned.1.call-start = ((), (), s32[]{:S(2)}) async-start(), calls=%async_computation.6 | async-start | bytes 2129920 | tf_op jit(solution)/shard_map/all_gather | solution.py:162
  323.1 42.5 %copy-start.38 = (f32[256]{0:T(256)S(1)}, f32[256]{0:T(256)}, u32[]{:S(2)}) copy-start(f32[256]{0:T(256)} %param.36) | copy-start | bytes 3076
  323.2 43.0 %copy-start.36 = (f32[512]{0:T(512)S(1)}, f32[512]{0:T(512)}, u32[]{:S(2)}) copy-start(f32[512]{0:T(512)} %param.34) | copy-start | bytes 6148
  561.5 3.3 copy-start.7
  562.9 5.3 copy-start.15
  564.8 3.4 copy-start.13
  564.8 5.1 copy-start.10
  568.2 3.0 copy-start.5
  (15 other events, 24.0 us)
Sparse Core Ops, SparseCore 0:
  9.5 32.7 all-gather.2
  292.7 29.1 reduce-scatter.1
  328.9 230.5 all-reduce.4
  561.5 19.5 all-gather.4
where the time goes:
time: 592 us; the launch traced here: 591 us
  waiting for transfers between devices  296 us (50%)
  local copies, waits for them, and re-layouts  130 us (22%)
  other arithmetic  59.6 us (10%)
  blocking collectives  40.8 us (7%)
  matrix products  34 us (6%)
  starting transfers between devices  15.7 us (3%)
  between operations  14.4 us (2%)
    psum x1, waiting for transfers between devices, body(): summed = lax.psum(r_part, ('group', 'local'))  192 us
    psum x1, blocking collectives, body(): lax.psum((grads[0][0], grads[0][1], grads[1][0], grads[1][1], grads[2][0]...  40.8 us
    scatter-add x1, other arithmetic, body(): jax.ops.segment_sum(returned, served_flat, num_segments=segment_count)  40.3 us
    all_to_all x1, waiting for transfers between devices, body(): lax.all_to_all(outbound.astype(jnp.bfloat16), 'group', split_axis=0, conc...  39.2 us
    all_to_all x1, waiting for transfers between devices, body(): lax.all_to_all(served_rows, 'group', split_axis=0, concat_axis=0, tiled=T...  38.3 us
    gather x1, local copies, waits for them, and re-layouts, body(): outgoing = keys_padded[source].reshape(groups, capacity)  34.5 us
    scatter x1, local copies, waits for them, and re-layouts, pair_back(): spread = jnp.zeros((vectors_all.shape[0], vectors, vectors), jnp.float32)...  19 us
    gather x1, local copies, waits for them, and re-layouts, body(): outbound = grad_padded[source].reshape(groups, capacity, embed_width)  15.5 us
  transfers between devices with their start and end apart: 7, of which 6 were waited for; matrix products, arithmetic and copies ran while one was open for 18% of the time, Pallas kernels for 0%

commit v1 on v0

--- a/solution.py
+++ b/solution.py
@@ -166,7 +166,10 @@
         (d_embed * q_val).reshape(batch_rows, table_count, embed_width),
         precision=highest,
     )
-    summed = lax.psum(r_part, ("group", "local"))
+    begin_the_cubes = lambda x_part, device_axis, link_axis: lax.psum(
+        lax.psum(x_part, link_axis), device_axis
+    )
+    summed = begin_the_cubes(r_part, "group", "local")
     r_grad = lax.dynamic_slice_in_dim(
         summed, lax.axis_index("local") * r_tables.shape[0], r_tables.shape[0], 0
     )

time: 592 us -> 683 us (1.15)
  waiting for transfers between devices: 296 us -> 386 us
    psum x1 -> x3, waiting for transfers between devices: 192 us -> 272 us  [the longest x1 144 us: body(): lax.psum((grads[0][0], grads[0][1], grads[1][0], grads[1][1], grads[2][0]...]
    all_gather x1, waiting for transfers between devices: 7.17 us -> 18.1 us  [body(): lax.all_gather(own_rows - table_rate * q_piece, 'local', axis=0, tiled=True)]
    all_to_all x1, waiting for transfers between devices: 39.2 us -> 30.5 us  [body(): lax.all_to_all(outbound.astype(jnp.bfloat16), 'group', split_axis=0, conc...]
    reduce_scatter x1, waiting for transfers between devices: 14.6 us -> 21.6 us  [body(): lax.psum_scatter(q_part.astype(jnp.bfloat16), 'local', scatter_dimension=...]
    unnamed x87 -> x83, local copies, waits for them, and re-layouts: 14.2 us -> 14.8 us
  transfers between devices with their start and end apart: 7 -> 9, of which waited for: 6 -> 7; matrix products, arithmetic and copies ran while one was open for 18% -> 22% of each run, Pallas kernels for 0% -> 0%
where the time goes in v1:
time: 683 us; the launch traced here: 682 us
  waiting for transfers between devices  386 us (57%)
  local copies, waits for them, and re-layouts  131 us (19%)
  other arithmetic  59.9 us (9%)
  blocking collectives  41.2 us (6%)
  matrix products  33.6 us (5%)
  starting transfers between devices  15.8 us (2%)
  between operations  14.7 us (2%)
    psum x1, waiting for transfers between devices, body(): lax.psum((grads[0][0], grads[0][1], grads[1][0], grads[1][1], grads[2][0]...  144 us
    psum x1, waiting for transfers between devices, body(): lax.psum(lax.psum(x_part, link_axis), device_axis)  128 us
    psum x1, blocking collectives, body(): lax.psum((grads[0][0], grads[0][1], grads[1][0], grads[1][1], grads[2][0]...  41.2 us
    scatter-add x1, other arithmetic, body(): jax.ops.segment_sum(returned, served_flat, num_segments=segment_count)  39.7 us
    all_to_all x1, waiting for transfers between devices, body(): lax.all_to_all(served_rows, 'group', split_axis=0, concat_axis=0, tiled=T...  38.3 us
    gather x1, local copies, waits for them, and re-layouts, body(): outgoing = keys_padded[source].reshape(groups, capacity)  34.5 us
    all_to_all x1, waiting for transfers between devices, body(): lax.all_to_all(outbound.astype(jnp.bfloat16), 'group', split_axis=0, conc...  30.5 us
    reduce_scatter x1, waiting for transfers between devices, body(): lax.psum_scatter(q_part.astype(jnp.bfloat16), 'local', scatter_dimension=...  21.6 us
  transfers between devices with their start and end apart: 9, of which 7 were waited for; matrix products, arithmetic and copies ran while one was open for 22% of the time, Pallas kernels for 0%

profile of v1, /device:TPU:0, one launch (start us, length us, event | category | flops | bytes accessed | tf_op | source)
XLA Modules:
  0.0 682.2 jit_solution(12099447482446068399)
XLA Ops:
  11.3 12.8 %scatter_custom_fusion = s32[6656]{0:T(1024)S(1)} fusion(s32[3328]{0:T(1024)S(1)} %fusion.38, s32[3328]{0:T(1024)S(1)} %iota.29, s32[]{:T(128)} %constant.27.clone.1), kind=kCustom, calls=%fused_computation.84 | custom fusion | bytes 26628 | tf_op jit(solution)/shard_map/scatter | solution.py:117
  24.1 34.5 %gather_fusion = s32[6656]{0:T(1024)S(1)} fusion(s32[3329]{0:T(1024)S(1)} %pad_add_fusion, s32[7168]{0:T(1024)S(1)} %pad_clamp_fusion.1), kind=kCustom, calls=%fused_computation | custom fusion | bytes 79872 | tf_op jit(solution)/shard_map/gather | solution.py:121
  59.3 7.3 %all-to-all-start = ((s32[8,1,832]{2,1,0:T(1,128)}), s32[8,1,832]{2,1,0:T(1,128)S(1)}, u32[]{:S(2)}, u32[]{:S(2)}) async-start(s32[8,1,832]{2,1,0:T(1,128)} %all_to_all.14), calls=%async_computation | async-start | bytes 57344 | tf_op jit(solution)/shard_map/all_to_all | solution.py:123
  66.6 2.5 copy.64
  69.3 4.0 all-to-all-done
  73.5 14.3 %gather_fusion.1 = bf16[6656,128]{1,0:T(8,128)(2,1)} fusion(bf16[3328,128]{1,0:T(8,128)(2,1)S(1)} %reshape.127, s32[7168]{0:T(1024)S(1)} %pad_clamp_fusion), kind=kCustom, calls=%fused_computation.1 | custom fusion | bytes 3434496 | tf_op jit(solution)/shard_map/gather | solution.py:124
  87.7 3.8 all-to-all-start.1
  91.7 38.3 %all-to-all-done.1 = bf16[8,832,128]{2,1,0:T(8,128)(2,1)S(1)} async-done(((bf16[8,832,128]{2,1,0:T(8,128)(2,1)}), bf16[8,832,128]{2,1,0:T(8,128)(2,1)S(1)}, u32[]{:S(2)}, u32[]{:S(2)}) %all-to-all-start.1) | async-done | bytes 1703968 | tf_op jit(solution)/shard_map/all_to_all | solution.py:125
  129.9 6.5 gather_fusion.2
  137.2 7.3 %fusion.5 = (bf16[128,26,128]{2,0,1:T(8,128)(2,1)S(1)}, f32[26,128,128]{2,1,0:T(8,128)}) fusion(f32[128,26,128]{2,1,0:T(8,128)S(1)} %reshape.131, f32[256,26,128]{2,0,1:T(8,128)} %all-gather.3.cloned.1.call-done, s32[128,26]{0,1:T(8,128)S(1)} %copy-done.25), kind=kOutput, calls=%fused_computation.19 | convolution fusion | flops 1310326784 | bytes 7681024 | tf_op jit(solution)/shard_map/btr,rtd->btd/dot_general | solution.py:132
  146.4 4.9 gather_fusion.3
  151.7 2.3 convolution_add_fusion.1
  159.5 19.0 %scatter_fusion = f32[128,27,27]{0,2,1:T(8,128)S(1)} fusion(f32[128,27,27]{0,2,1:T(8,128)S(1)} %broadcast_in_dim.21, s32[351]{0:T(512)S(1)} %copy-done, f32[351,128]{1,0:T(8,128)S(1)} %convolution_bitcast_fusion), kind=kCustom, calls=%fused_computation.6 | custom fusion | bytes 541944 | tf_op jit(solution)/shard_map/scatter | solution.py:33
  178.8 2.9 copy.87
  181.7 3.3 fusion.14
  187.6 2.1 mul.158
  191.0 14.3 %gather_fusion.4 = bf16[6656,128]{1,0:T(8,128)(2,1)} fusion(bf16[3329,128]{1,0:T(8,128)(2,1)S(1)} %concatenate.24, s32[7168]{0:T(1024)S(1)} %pad_clamp_fusion.1), kind=kCustom, calls=%fused_computation.4 | custom fusion | bytes 3434496 | tf_op jit(solution)/shard_map/gather | solution.py:145
  205.2 4.4 all-to-all-start.2
  209.7 7.9 %fusion.4 = f32[256,26,128]{0,2,1:T(8,128)} fusion(s32[128,26]{0,1:T(8,128)S(1)} %copy-done.26, f32[128,26,128]{2,1,0:T(8,128)S(1)} %fusion.14, f32[128,26,128]{2,1,0:T(8,128)} %copy-done.1), kind=kOutput, calls=%fused_computation.16 | convolution fusion | flops 1309900800 | bytes 6829056 | tf_op jit(solution)/shard_map/btr,btd->rtd/dot_general | solution.py:163
  218.5 30.5 %all-to-all-done.2 = bf16[8,832,128]{2,1,0:T(8,128)(2,1)} async-done(((bf16[8,832,128]{2,1,0:T(8,128)(2,1)}), bf16[8,832,128]{2,1,0:T(8,128)(2,1)}, u32[]{:S(2)}, u32[]{:S(2)}) %all-to-all-start.2) | async-done | bytes 1703968 | tf_op jit(solution)/shard_map/all_to_all | solution.py:147
  249.0 39.7 %scatter_custom_fusion.2 = f32[3328,128]{1,0:T(8,128)S(1)} fusion(s32[6656]{0:T(1024)S(1)} %reshape.188, bf16[6656,128]{1,0:T(8,128)(2,1)} %bitcast.13, f32[]{:T(128)} %constant.24.clone.1), kind=kCustom, calls=%fused_computation.9 | custom fusion | flops 1703936 | bytes 3407876 | tf_op jit(solution)/shard_map/scatter-add | solution.py:154
  294.8 2.8 fusion.24
  298.2 21.6 %reduce-scatter.2.cloned.1.call-done = bf16[32,26,128]{2,1,0:T(8,128)(2,1)} async-done(((bf16[128,26,128]{2,1,0:T(8,128)(2,1)}), bf16[32,26,128]{2,1,0:T(8,128)(2,1)}) %reduce-scatter.2.cloned.1.call-update) | async-done | bytes 213008 | tf_op jit(solution)/shard_map/reduce_scatter | solution.py:157
  323.6 41.2 %all-reduce.1 = (f32[1024]{0:T(1024)S(1)}, f32[1024]{0:T(1024)S(1)}, f32[512]{0:T(512)S(1)}, f32[256]{0:T(256)S(1)}) all-reduce(f32[1024]{0:T(1024)S(1)} %copy-done.34, f32[1024]{0:T(1024)S(1)} %copy-done.33, f32[512]{0:T(512)} %get-tuple-element.54, ...), channel_id=1, replica_groups=mesh['group'=8,'local'=4] {'group','local'}, use_global_device_ids=true, to_apply=%region_10.11 | all-reduce | flops 2816 | bytes 22528 | tf_op jit(solution)/shard_map/psum | solution.py:177
  367.9 143.7 %all-reduce.11.cloned.1.call-done = (f32[479,1024]{1,0:T(8,128)}, f32[1024,1024]{1,0:T(8,128)}, f32[1024,512]{1,0:T(8,128)}, f32[512,256]{1,0:T(8,128)}) async-done(((f32[479,1024]{1,0:T(8,128)}, f32[1024,1024]{1,0:T(8,128)}, f32[1024,512]{1,0:T(8,128)}, f32[512,256]{1,0:T(8,128)}), (f32[479,1024]{1,0:T(8,128)}, f32[1024,1024]{1,0:T(8,128)}, f32[1024,512]{1,0:T(8,128)}, ...) | async-done | bytes 8777744 | tf_op jit(solution)/shard_map/psum | solution.py:177
  511.6 2.1 multiply_subtract_fusion.4
  513.7 3.4 multiply_subtract_fusion.2
  520.0 2.7 multiply_subtract_fusion
  522.8 128.4 %all-reduce.9.cloned.1.call-done = f32[256,26,128]{0,2,1:T(8,128)} async-done(((f32[256,26,128]{0,2,1:T(8,128)}), f32[256,26,128]{0,2,1:T(8,128)}) %all-reduce.9.cloned.1.call-update) | async-done | bytes 3407888 | tf_op jit(solution)/shard_map/psum | solution.py:169
  651.1 2.0 multiply_subtract_fusion.3
  654.5 18.1 %all-gather.5.cloned.1.call-done = f32[128,26,128]{2,0,1:T(8,128)} async-done(((f32[32,26,128]{2,0,1:T(8,128)}), f32[128,26,128]{2,0,1:T(8,128)}) %all-gather.5.cloned.1.call-update) | async-done | bytes 1703952 | tf_op jit(solution)/shard_map/all_gather | solution.py:162
  672.5 2.8 copy.113
  (147 shorter events, 36.3 us)
Async XLA Ops:
  7.2 129.5 %all-gather.3.cloned.1.call-start = ((), (), s32[]{:S(2)}) async-start(), calls=%async_computation.4 | async-start | bytes 4259840 | tf_op jit(solution)/shard_map/all_gather | solution.py:127
  59.3 14.0 %all-to-all-start = ((s32[8,1,832]{2,1,0:T(1,128)}), s32[8,1,832]{2,1,0:T(1,128)S(1)}, u32[]{:S(2)}, u32[]{:S(2)}) async-start(s32[8,1,832]{2,1,0:T(1,128)} %all_to_all.14), calls=%async_computation | async-start | bytes 57344 | tf_op jit(solution)/shard_map/all_to_all | solution.py:123
  69.1 18.6 %copy-start.2 = (f32[128,26,128]{2,1,0:T(8,128)}, f32[128,26,128]{2,1,0:T(8,128)S(1)}, u32[]{:S(2)}) copy-start(f32[128,26,128]{2,1,0:T(8,128)S(1)} %copy.64) | copy-start | bytes 5111812
  73.3 14.4 %copy-start.20 = (s32[8,1,832]{2,1,0:T(1,128)}, s32[8,1,832]{2,1,0:T(1,128)S(1)}, u32[]{:S(2)}) copy-start(s32[8,1,832]{2,1,0:T(1,128)S(1)} %all-to-all-done) | copy-start | bytes 79876
  87.7 3.8 copy-start.22
  87.7 42.2 %all-to-all-start.1 = ((bf16[8,832,128]{2,1,0:T(8,128)(2,1)}), bf16[8,832,128]{2,1,0:T(8,128)(2,1)S(1)}, u32[]{:S(2)}, u32[]{:S(2)}) async-start(bf16[8,832,128]{2,1,0:T(8,128)(2,1)} %bitcast.55), calls=%async_computation.1 | async-start | bytes 3407872 | tf_op jit(solution)/shard_map/all_to_all | solution.py:125
  136.7 7.8 %copy-start.1 = (f32[128,26,128]{2,1,0:T(8,128)}, f32[128,26,128]{2,1,0:T(8,128)S(1)}, u32[]{:S(2)}) copy-start(f32[128,26,128]{2,1,0:T(8,128)S(1)} %reshape.131) | copy-start | bytes 5111812
  144.6 6.7 copy-start.5
  144.6 6.7 copy-start.29
  145.3 6.4 copy-start.31
  151.6 5.4 copy-start.10
  155.9 3.1 copy-start.23
  159.1 19.4 %copy-start.18 = (bf16[128,1024]{1,0:T(8,128)(2,1)}, bf16[128,1024]{1,0:T(8,128)(2,1)S(1)}, u32[]{:S(2)}) copy-start(bf16[128,1024]{1,0:T(8,128)(2,1)S(1)} %get-tuple-element.51) | copy-start | bytes 786436
  181.7 3.3 copy-start.3
  205.2 4.5 copy-start.26
  205.2 43.8 %all-to-all-start.2 = ((bf16[8,832,128]{2,1,0:T(8,128)(2,1)}), bf16[8,832,128]{2,1,0:T(8,128)(2,1)}, u32[]{:S(2)}, u32[]{:S(2)}) async-start(bf16[8,832,128]{2,1,0:T(8,128)(2,1)} %bitcast.54), calls=%async_computation.2 | async-start | bytes 3407872 | tf_op jit(solution)/shard_map/all_to_all | solution.py:147
  209.7 88.0 %all-reduce.7.cloned.1.call-start = ((), (), s32[]{:S(2)}) async-start(), calls=%async_computation.7 | async-start | bytes 6815744 | tf_op jit(solution)/shard_map/psum | solution.py:170
  217.7 102.2 %reduce-scatter.2.cloned.1.call-start = ((), (), s32[]{:S(2)}) async-start(), calls=%async_computation.5 | async-start | bytes 1310720 | tf_op jit(solution)/shard_map/reduce_scatter | solution.py:157
  290.1 2.9 copy-start.16
  290.1 2.9 copy-start.24
  290.1 221.5 %all-reduce.11.cloned.1.call-start = ((), (), s32[]{:S(2)}) async-start(), calls=%async_computation.9 | async-start | bytes 17563648 | tf_op jit(solution)/shard_map/psum | solution.py:177
  291.3 3.5 copy-start.11
  297.6 353.6 %all-reduce.9.cloned.1.call-start = ((), (), s32[]{:S(2)}) async-start(), calls=%async_computation.8 | async-start | bytes 6815744 | tf_op jit(solution)/shard_map/psum | solution.py:169
  298.2 24.0 %copy-start.7 = (f32[64,26,128]{2,0,1:T(8,128)S(1)}, f32[64,26,128]{2,0,1:T(8,128)}, u32[]{:S(2)}) copy-start(f32[64,26,128]{2,0,1:T(8,128)} %param.25) | copy-start | bytes 2555908
  298.2 374.4 %all-gather.5.cloned.1.call-start = ((), (), s32[]{:S(2)}) async-start(), calls=%async_computation.6 | async-start | bytes 2129920 | tf_op jit(solution)/shard_map/all_gather | solution.py:162
  321.1 46.2 %copy-start.30 = (f32[1024]{0:T(1024)S(1)}, f32[1024]{0:T(1024)}, u32[]{:S(2)}) copy-start(f32[1024]{0:T(1024)} %param.30) | copy-start | bytes 12292
  321.1 46.2 %copy-start.32 = (f32[1024]{0:T(1024)S(1)}, f32[1024]{0:T(1024)}, u32[]{:S(2)}) copy-start(f32[1024]{0:T(1024)} %param.32) | copy-start | bytes 12292
  322.2 191.5 %copy-start.6 = (bf16[479,1024]{1,0:T(8,128)(2,1)S(1)}, bf16[479,1024]{1,0:T(8,128)(2,1)}, u32[]{:S(2)}) copy-start(bf16[479,1024]{1,0:T(8,128)(2,1)} %param.29) | copy-start | bytes 2942980
  511.6 5.5 copy-start.14
  513.7 3.4 copy-start.12
  513.7 5.1 copy-start.9
  517.1 2.9 copy-start.4
  (15 other events, 24.6 us)
Sparse Core Ops, SparseCore 0:
  9.5 32.7 all-gather.2
  217.8 73.9 all-reduce.6
  294.9 24.9 reduce-scatter.1
  326.6 184.9 all-reduce.10
  515.1 135.9 all-reduce.8
  653.1 19.3 all-gather.4
